TPU v7x, 32 devices: a whole 2x2x4 slice. The times are simulated.
32 devices in a mesh: gx: 4 (over z), gy: 4 (over x, core), gz: 2 (over y).
Axes of the slice: x: 2, y: 2, z: 4, core: 2. Of those that a mesh axis runs over, the one named last changes fastest.
Arguments:
- volume: int32 [32, 64, 256], P('gx', 'gy', 'gz'), may hold values from 0 to 255
- transfer_table: float32 [4, 256], replicated, may hold values from 0 to 1
- depth_rank: int32 [4], replicated, may hold values from 0 to 3, each once
- footprint: int32 [4, 4, 2, 4], P('gx', 'gy', 'gz'), may hold values from 0 to 128, as said below
Outputs:
- rendered: float32 [4, 64, 256], P(None, 'gy', 'gz')
Inputs may be any that keep to these rules, and one draw needn't show every extreme that they name: depth_rank holds each of 0 to 4 - 1 once. `footprint`: for every brick, entry 0 is below 8 and entry 1 above it, up to 16; entry 2 is below 64 and entry 3 above it, up to 128.
All inputs are finite; a program needn't handle non-finite values.
Results may differ from a plain program's by a relative error of at most 0.0003.
Values sent between devices are 32-bit elements; how exact they have to be, the bound alone decides.
A program may use at most 64 MiB of HBM per device.

v0:
```python
import functools

import jax
import jax.numpy as jnp
from jax import lax
from jax.experimental import pallas as pl
from jax.experimental.pallas import tpu as pltpu
from jax.sharding import PartitionSpec as P

LIGHT = (1.0 / 3.0, 2.0 / 3.0, 2.0 / 3.0)
AXES = ("gx", "gy", "gz")
MESH = pl.DeviceIdType.MESH


def lookup(table_row, index, lanes):
    entries = table_row.shape[1]
    low = index & (lanes - 1)
    found = None
    for part in range(entries // lanes):
        piece = jnp.broadcast_to(table_row[:, part * lanes:(part + 1) * lanes], index.shape)
        got = jnp.take_along_axis(piece, low, axis=1, mode="promise_in_bounds")
        found = got if found is None else jnp.where(index >= part * lanes, got, found)
    return found


def kernel(sizes, vol_hbm, table_hbm, rank_hbm, foot_hbm, out_ref,
           vol_ref, table_ref, rank_ref, foot_ref, load_sem, dens, wemit, inner, edge, xh, yh, zh, alphas, colours,
           halo_send, halo_recv, a_send, a_recv, c_send, c_recv):
    n, ny, nz = sizes
    depth, rows, lanes = vol_ref.shape
    extent = 4.0 / (depth * n)
    me = [lax.axis_index(a) for a in AXES]
    ix = me[0]

    barrier = pltpu.get_barrier_semaphore()
    for off in range(1, n):
        pl.semaphore_signal(barrier, inc=1, device_id={"gx": lax.rem(ix + off, n)}, device_id_type=MESH)
    for a in (1, 2):
        if sizes[a] > 1:
            @pl.when(me[a] > 0)
            def _():
                pl.semaphore_signal(barrier, inc=1, device_id={AXES[a]: me[a] - 1}, device_id_type=MESH)

            @pl.when(me[a] < sizes[a] - 1)
            def _():
                pl.semaphore_signal(barrier, inc=1, device_id={AXES[a]: me[a] + 1}, device_id_type=MESH)

    loads = [
        pltpu.make_async_copy(src, dst, load_sem.at[i])
        for i, (src, dst) in enumerate((
            (vol_hbm, vol_ref), (table_hbm, table_ref), (foot_hbm, foot_ref), (rank_hbm, rank_ref)
        ))
    ]
    for load in loads:
        load.start()
    loads[0].wait()
    loads[1].wait()

    lane = lax.broadcasted_iota(jnp.int32, (8, lanes), 1)
    vol = vol_ref[...].reshape(depth * rows, lanes)
    d_all = lookup(table_ref[3:4, :], vol, lanes)
    d3 = d_all.reshape(depth, rows, lanes)
    dens[...] = d3
    edge[0] = d3[:, 0, :]
    edge[1] = d3[:, rows - 1, :]
    first = jnp.zeros((8, lanes), jnp.float32)
    last = jnp.zeros((8, lanes), jnp.float32)
    groups = depth * rows // 8
    for v in range(groups):
        piece = d_all[v * 8:(v + 1) * 8]
        to_last = (2 * v + 1) % lanes
        to_first = (2 * v - 1) % lanes
        last = jnp.where(lane == 2 * v, pltpu.roll(piece, to_last, 1) if to_last else piece, last)
        first = jnp.where(lane == to_first, pltpu.roll(piece, to_first, 1) if to_first else piece, first)
    edge[2] = first
    edge[3] = last

    sources = (
        (dens.at[0], dens.at[depth - 1]),
        (edge.at[0], edge.at[1]),
        (edge.at[2], edge.at[3]),
    )
    halos = (xh, yh, zh)

    def halo_copy(a, upward):
        slot = 0 if upward else 1
        return pltpu.make_async_remote_copy(
            src_ref=sources[a][1 if upward else 0],
            dst_ref=halos[a].at[slot],
            send_sem=halo_send.at[a, slot],
            recv_sem=halo_recv.at[a, slot],
            device_id={AXES[a]: me[a] + (1 if upward else -1)},
            device_id_type=MESH,
        )

    greeted = n - 1
    for a in (1, 2):
        greeted = greeted + lax.min(me[a], 1) + lax.min(sizes[a] - 1 - me[a], 1)
    pl.semaphore_wait(barrier, greeted)

    for a in (1, 2, 0):
        @pl.when(me[a] < sizes[a] - 1)
        def _():
            halo_copy(a, True).start()

        @pl.when(me[a] == 0)
        def _():
            halos[a][0] = jnp.zeros(halos[a].shape[1:], jnp.float32)

        @pl.when(me[a] > 0)
        def _():
            halo_copy(a, False).start()

        @pl.when(me[a] == sizes[a] - 1)
        def _():
            halos[a][1] = jnp.zeros(halos[a].shape[1:], jnp.float32)

    loads[2].wait()
    row_no = lax.broadcasted_iota(jnp.int32, (rows, lanes), 0)
    lane_no = lax.broadcasted_iota(jnp.int32, (rows, lanes), 1)
    inside = (
        (row_no >= foot_ref[0, 0, 0, 0])
        & (row_no < foot_ref[0, 0, 0, 1])
        & (lane_no >= foot_ref[0, 0, 0, 2])
        & (lane_no < foot_ref[0, 0, 0, 3])
    )

    transmit = jnp.ones((rows, lanes), jnp.float32)
    weights = []
    for x in range(depth):
        sample = 1.0 - jnp.exp(-extent * d3[x])
        weights.append(transmit * sample)
        transmit = transmit * (1.0 - sample)
    alphas[ix] = jnp.where(inside, 1.0 - transmit, 0.0)

    def image_copy(buf, off, s_sem, r_sem):
        return pltpu.make_async_remote_copy(
            src_ref=buf.at[ix],
            dst_ref=buf.at[ix],
            send_sem=s_sem.at[off],
            recv_sem=r_sem.at[off],
            device_id={"gx": lax.rem(ix + off, n)},
            device_id_type=MESH,
        )

    def send_images(buf, s_sem, r_sem):
        for far in range(n - 1, 0, -1):
            @pl.when(ix + far < n)
            def _():
                image_copy(buf, far, s_sem, r_sem).start()

            @pl.when(ix - far >= 0)
            def _():
                image_copy(buf, n - far, s_sem, r_sem).start()

    send_images(alphas, a_send, a_recv)

    for c in range(3):
        emit = lookup(table_ref[c:c + 1, :], vol, lanes).reshape(depth, rows, lanes)
        for x in range(depth):
            wemit[c, x] = weights[x] * emit[x]

    per = rows // 8
    for x in range(depth):
        d = d3[x]
        up = jnp.where(row_no == 0, 0.0, pltpu.roll(d, 1, 0))
        down = jnp.where(row_no == rows - 1, 0.0, pltpu.roll(d, rows - 1, 0))
        inner[0, x] = 0.5 * (down - up)
        left = jnp.where(lane_no == 0, 0.0, pltpu.roll(d, 1, 1))
        right = jnp.where(lane_no == lanes - 1, 0.0, pltpu.roll(d, lanes - 1, 1))
        inner[1, x] = 0.5 * (right - left)
    line = lax.broadcasted_iota(jnp.int32, (8, lanes), 0)
    on_side = (lane == 0) | (lane == lanes - 1)

    for a in range(3):
        @pl.when(me[a] > 0)
        def _():
            halo_copy(a, True).wait_recv()

        @pl.when(me[a] < sizes[a] - 1)
        def _():
            halo_copy(a, False).wait_recv()

    sides = 0.5 * (zh[1] - zh[0])
    half_up = 0.5 * yh[0]
    half_down = 0.5 * yh[1]
    layers = [xh.at[0]] + [dens.at[x] for x in range(depth)] + [xh.at[1]]
    colour = [[None] * per for _ in range(3)]
    for x in range(depth):
        for h in range(per):
            at = pl.ds(h * 8, 8)
            v = x * per + h
            g_x = 0.5 * (layers[x + 2][at, :] - layers[x][at, :])
            g_y = inner[0, x, at, :]
            if h == 0:
                g_y = jnp.where(line == 0, g_y - half_up[x:x + 1, :], g_y)
            if h == per - 1:
                g_y = jnp.where(line == 7, g_y + half_down[x:x + 1, :], g_y)
            side = pltpu.roll(sides, lanes - 2 * v, 1) if v else sides
            g_z = inner[1, x, at, :]
            g_z = jnp.where(on_side, g_z + side, g_z)
            facing = jnp.abs(g_x * LIGHT[0] + g_y * LIGHT[1] + g_z * LIGHT[2]) * lax.rsqrt(
                1.0 + (g_x * g_x + g_y * g_y + g_z * g_z)
            )
            shade = 0.35 + 0.65 * facing
            for c in range(3):
                term = wemit[c, x, at, :] * shade
                colour[c][h] = term if x == 0 else colour[c][h] + term
    colour = [jnp.concatenate(c, axis=0) for c in colour]
    for c in range(3):
        colours[ix, c] = jnp.where(inside, colour[c], 0.0)

    send_images(colours, c_send, c_recv)

    loads[3].wait()
    order = []
    for p in range(n):
        at = 0
        for i in range(n):
            at = jnp.where(rank_ref[i] == p, i, at)
        order.append(at)

    for off in range(1, n):
        image_copy(alphas, off, a_send, a_recv).wait_recv()
    covers = []
    alpha = jnp.zeros((rows, lanes), jnp.float32)
    for p in range(n):
        covers.append(1.0 - alpha)
        alpha = alpha + covers[p] * alphas[order[p]]
    out_ref[3] = alpha
    for a in range(3):
        @pl.when(me[a] < sizes[a] - 1)
        def _():
            halo_copy(a, True).wait_send()

        @pl.when(me[a] > 0)
        def _():
            halo_copy(a, False).wait_send()
    for off in range(1, n):
        image_copy(alphas, off, a_send, a_recv).wait_send()

    for off in range(1, n):
        image_copy(colours, off, c_send, c_recv).wait_recv()
    total = [None] * 3
    for p in range(n):
        for c in range(3):
            term = covers[p] * colours[order[p], c]
            total[c] = term if p == 0 else total[c] + term
    for c in range(3):
        out_ref[c] = total[c]
    for off in range(1, n):
        image_copy(colours, off, c_send, c_recv).wait_send()


def on_device(sizes, volume, transfer_table, depth_rank, footprint):
    depth, rows, lanes = volume.shape
    n = sizes[0]
    vmem = pl.BlockSpec(memory_space=pltpu.VMEM)
    hbm = pl.BlockSpec(memory_space=pl.ANY)
    return pl.pallas_call(
        functools.partial(kernel, sizes),
        out_shape=pltpu.VMEM((4, rows, lanes), jnp.float32),
        in_specs=[hbm] * 4,
        out_specs=vmem,
        scratch_shapes=[
            pltpu.VMEM(volume.shape, jnp.int32),
            pltpu.VMEM(transfer_table.shape, jnp.float32),
            pltpu.SMEM(depth_rank.shape, jnp.int32),
            pltpu.SMEM(footprint.shape, jnp.int32),
            pltpu.SemaphoreType.DMA((4,)),
            pltpu.VMEM((depth, rows, lanes), jnp.float32),
            pltpu.VMEM((3, depth, rows, lanes), jnp.float32),
            pltpu.VMEM((2, depth, rows, lanes), jnp.float32),
            pltpu.VMEM((4, 8, lanes), jnp.float32),
            pltpu.VMEM((2, rows, lanes), jnp.float32),
            pltpu.VMEM((2, depth, lanes), jnp.float32),
            pltpu.VMEM((2, 8, lanes), jnp.float32),
            pltpu.VMEM((n, rows, lanes), jnp.float32),
            pltpu.VMEM((n, 3, rows, lanes), jnp.float32),
            pltpu.SemaphoreType.DMA((3, 2)),
            pltpu.SemaphoreType.DMA((3, 2)),
            pltpu.SemaphoreType.DMA((n,)),
            pltpu.SemaphoreType.DMA((n,)),
            pltpu.SemaphoreType.DMA((n,)),
            pltpu.SemaphoreType.DMA((n,)),
        ],
        compiler_params=pltpu.CompilerParams(collective_id=0, has_side_effects=True),
        name="raycast",
    )(volume, transfer_table, depth_rank, footprint)


def solution(mesh):
    placed = (P("gx", "gy", "gz"), P(), P(), P("gx", "gy", "gz", None))
    sizes = tuple(mesh.shape[a] for a in AXES)
    return jax.shard_map(
        functools.partial(on_device, sizes), mesh=mesh, in_specs=placed,
        out_specs=P(None, "gy", "gz"), check_vma=False,
    )
```

profile of v0, /device:TPU:0, one launch (start us, length us, event | category | flops | bytes accessed | tf_op | source)
XLA Modules:
  0.0 12.5 jit_solution(15786446881382230854)
XLA Ops:
  0.0 11.8 %raycast.1 = f32[4,16,128]{2,1,0:T(8,128)S(1)} custom-call(s32[8,16,128]{2,1,0:T(8,128)} %vol_hbm.1, f32[4,256]{1,0:T(4,128)} %table_hbm.1, s32[4]{0:T(128)} %rank_hbm.1, s32[1,1,1,4]{3,2,1,0:T(1,128)} %foot_hbm.1), custom_call_target="tpu_custom_call" | custom-call | tf_op jit(solution)/shard_map/raycast/pallas_call | solution.py:260
  11.9 0.6 %copy.6 = f32[4,16,128]{2,1,0:T(8,128)} copy(f32[4,16,128]{2,1,0:T(8,128)S(1)} %raycast.1) | data formatting | bytes 65536
where the time goes:
time: 12.6 us; the launch traced here: 12.5 us
  Pallas kernels  11.8 us (94%)
  local copies, waits for them, and re-layouts  0.62 us (5%)
    pallas_call x1, Pallas kernels, on_device(): pl.pallas_call(functools.partial(kernel, sizes), out_shape=pltpu.VMEM((4,...  11.8 us
    unnamed x1, local copies, waits for them, and re-layouts  0.62 us

commit v1 on v0

v1 whole, which is shorter than its diff:
```python
import functools

import jax
import jax.numpy as jnp
from jax import lax
from jax.experimental import pallas as pl
from jax.experimental.pallas import tpu as pltpu
from jax.sharding import PartitionSpec as P

LIGHT = (1.0 / 3.0, 2.0 / 3.0, 2.0 / 3.0)
AXES = ("gx", "gy", "gz")
MESH = pl.DeviceIdType.MESH
RAW = 1


def lookup(table_row, index, lanes):
    entries = table_row.shape[1]
    low = index & (lanes - 1)
    found = None
    for part in range(entries // lanes):
        piece = jnp.broadcast_to(table_row[:, part * lanes:(part + 1) * lanes], index.shape)
        got = jnp.take_along_axis(piece, low, axis=1, mode="promise_in_bounds")
        found = got if found is None else jnp.where(index >= part * lanes, got, found)
    return found


def kernel(sizes, vol_hbm, table_hbm, rank_hbm, foot_hbm, out_ref,
           vols, table_ref, rank_ref, foot_ref, load_sem, frames, yedge, zedge, xh, yh, zh,
           dens, wemit, inner, alphas, colours,
           ready, far_ready, halo_send, halo_recv, front_send, raw_recv, edge_recv, a_send, a_recv, c_send, c_recv):
    n, ny, nz = sizes
    _, depth, rows, lanes = vols.shape
    per = rows // 8
    extent = 4.0 / (depth * n)
    me = [lax.axis_index(a) for a in AXES]
    ix = me[0]
    raw_from = max(1, n - RAW)
    is_raw = ix >= raw_from
    has_lower = [me[a] > 0 for a in range(3)]
    has_upper = [me[a] < sizes[a] - 1 for a in range(3)]

    def signal(sem, **where):
        pl.semaphore_signal(sem, inc=1, device_id=where, device_id_type=MESH)

    barrier = pltpu.get_barrier_semaphore()
    for off in range(n - 1, 0, -1):
        @pl.when(ix + off < n)
        def _():
            signal(barrier, gx=ix + off)
    for a in (1, 2):
        if sizes[a] > 1:
            @pl.when(has_upper[a])
            def _():
                signal(barrier, **{AXES[a]: me[a] + 1})

            @pl.when((ix == 0) & has_upper[a])
            def _():
                for k in range(n - 1, 0, -1):
                    signal(barrier, **{"gx": k, AXES[a]: me[a] + 1})

    loads = [
        pltpu.make_async_copy(src, dst, load_sem.at[i])
        for i, (src, dst) in enumerate((
            (vol_hbm, vols.at[ix]), (table_hbm, table_ref), (foot_hbm, foot_ref), (rank_hbm, rank_ref)
        ))
    ]
    for load in loads:
        load.start()

    greeted = ix
    for a in (1, 2):
        greeted = greeted + lax.min(me[a], 1) * (1 + lax.min(ix, 1))

    @pl.when(greeted > 0)
    def _():
        pl.semaphore_wait(barrier, greeted)

    for a in range(3):
        if sizes[a] > 1:
            @pl.when(has_lower[a])
            def _():
                signal(ready, **{AXES[a]: me[a] - 1})
    for off in range(2, n):
        @pl.when(ix - off >= 0)
        def _():
            signal(far_ready, gx=ix - off)

    @pl.when(ix == 0)
    def _():
        xh[0] = jnp.zeros(xh.shape[1:], jnp.int32)

    @pl.when(ix == n - 1)
    def _():
        xh[1] = jnp.zeros(xh.shape[1:], jnp.int32)
    for a, halo in ((1, yh), (2, zh)):
        @pl.when(me[a] == 0)
        def _():
            halo[:, 0] = jnp.zeros((n,) + halo.shape[2:], jnp.int32)

        @pl.when(me[a] == sizes[a] - 1)
        def _():
            halo[:, 1] = jnp.zeros((n,) + halo.shape[2:], jnp.int32)

    lane = lax.broadcasted_iota(jnp.int32, (8, lanes), 1)
    line = lax.broadcasted_iota(jnp.int32, (8, lanes), 0)
    row_no = lax.broadcasted_iota(jnp.int32, (rows, lanes), 0)
    lane_no = lax.broadcasted_iota(jnp.int32, (rows, lanes), 1)

    loads[0].wait()
    vol3 = vols[ix]
    vol = vol3.reshape(depth * rows, lanes)
    yedge[0] = vol3[:, 0, :]
    yedge[1] = vol3[:, rows - 1, :]
    first = jnp.zeros((8, lanes), jnp.int32)
    last = jnp.zeros((8, lanes), jnp.int32)
    for v in range(depth * per):
        piece = vol[v * 8:(v + 1) * 8]
        to_last = (2 * v + 1) % lanes
        to_first = (2 * v - 1) % lanes
        last = jnp.where(lane == 2 * v, pltpu.roll(piece, to_last, 1) if to_last else piece, last)
        first = jnp.where(lane == to_first, pltpu.roll(piece, to_first, 1) if to_first else piece, first)
    zedge[0] = first
    zedge[1] = last
    sources = (
        (vols.at[ix, 0], vols.at[ix, depth - 1]),
        (yedge.at[0], yedge.at[1]),
        (zedge.at[0], zedge.at[1]),
    )

    def landing(a, side):
        return xh.at[1 - side] if a == 0 else (None, yh, zh)[a].at[ix, 1 - side]

    def halo_copy(a, side):
        return pltpu.make_async_remote_copy(
            src_ref=sources[a][side], dst_ref=landing(a, side),
            send_sem=halo_send.at[a, side], recv_sem=halo_recv.at[a, 1 - side],
            device_id={AXES[a]: me[a] + (1 if side else -1)}, device_id_type=MESH,
        )

    def edge_to_front(a, side):
        return pltpu.make_async_remote_copy(
            src_ref=sources[a][side], dst_ref=landing(a, side),
            send_sem=front_send.at[2 * a + side], recv_sem=edge_recv.at[ix, 2 * (a - 1) + 1 - side],
            device_id={"gx": 0, AXES[a]: me[a] + (1 if side else -1)}, device_id_type=MESH,
        )

    def raw_to_front():
        return pltpu.make_async_remote_copy(
            src_ref=vols.at[ix], dst_ref=vols.at[ix], send_sem=front_send.at[0], recv_sem=raw_recv.at[ix, 0],
            device_id={"gx": 0}, device_id_type=MESH,
        )

    def last_to_front():
        k = raw_from - 1
        return pltpu.make_async_remote_copy(
            src_ref=vols.at[k, depth - 1], dst_ref=vols.at[k, depth - 1],
            send_sem=front_send.at[0], recv_sem=raw_recv.at[k, 0],
            device_id={"gx": 0}, device_id_type=MESH,
        )

    def frame_to_front():
        return pltpu.make_async_remote_copy(
            src_ref=frames.at[ix], dst_ref=frames.at[ix], send_sem=front_send.at[1], recv_sem=raw_recv.at[ix, 1],
            device_id={"gx": 0}, device_id_type=MESH,
        )

    for a in (2, 1):
        @pl.when(is_raw & has_lower[a])
        def _():
            edge_to_front(a, 0).start()
    for a in (0, 2, 1):
        @pl.when(has_lower[a])
        def _():
            halo_copy(a, 0).start()

    if raw_from > 1:
        @pl.when(ix == raw_from - 1)
        def _():
            last_to_front().start()

    @pl.when(is_raw)
    def _():
        raw_to_front().start()

    loads[2].wait()
    frames[ix] = jnp.where(
        line == 0,
        ((lane >= foot_ref[0, 0, 0, 2]) & (lane < foot_ref[0, 0, 0, 3])).astype(jnp.int32),
        jnp.where(line == 1, foot_ref[0, 0, 0, 0], foot_ref[0, 0, 0, 1]),
    )

    @pl.when(is_raw)
    def _():
        frame_to_front().start()

    above = 0
    for a in range(3):
        above = above + lax.min(sizes[a] - 1 - me[a], 1)

    @pl.when(above > 0)
    def _():
        pl.semaphore_wait(ready, above)

    for a in (0, 2, 1):
        @pl.when(has_upper[a])
        def _():
            halo_copy(a, 1).start()
    for a in (2, 1):
        @pl.when(is_raw & has_upper[a])
        def _():
            edge_to_front(a, 1).start()

    loads[1].wait()

    def inside(b):
        frame = frames[b]
        return (frame[0:1] > 0) & (row_no >= frame[1:2]) & (row_no < frame[2:3])

    def prepare(b):
        ints = vols[b].reshape(depth * rows, lanes)
        d3 = lookup(table_ref[3:4, :], ints, lanes).reshape(depth, rows, lanes)
        dens[pl.ds(b * depth + 1, depth)] = d3
        transmit = jnp.ones((rows, lanes), jnp.float32)
        weights = []
        for x in range(depth):
            sample = 1.0 - jnp.exp(-extent * d3[x])
            weights.append(transmit * sample)
            transmit = transmit * (1.0 - sample)
        alphas[b] = jnp.where(inside(b), 1.0 - transmit, 0.0)
        for c in range(3):
            emit = lookup(table_ref[c:c + 1, :], ints, lanes).reshape(depth, rows, lanes)
            for x in range(depth):
                wemit[b, c, x] = weights[x] * emit[x]
        for x in range(depth):
            d = d3[x]
            up = jnp.where(row_no == 0, 0.0, pltpu.roll(d, 1, 0))
            down = jnp.where(row_no == rows - 1, 0.0, pltpu.roll(d, rows - 1, 0))
            inner[b, 0, x] = 0.5 * (down - up)
            left = jnp.where(lane_no == 0, 0.0, pltpu.roll(d, 1, 1))
            right = jnp.where(lane_no == lanes - 1, 0.0, pltpu.roll(d, lanes - 1, 1))
            inner[b, 1, x] = 0.5 * (right - left)

    half = [
        [jnp.where(has_lower[a], 0.5, 0.0), jnp.where(has_upper[a], 0.5, 0.0)] for a in range(3)
    ]
    even = (lane & 1) == 0
    on_side = (lane == 0) | (lane == lanes - 1)

    def shade(b, span):
        opacity = table_ref[3:4, :]
        half_up = half[1][0] * lookup(opacity, yh[b, 0], lanes)
        half_down = half[1][1] * lookup(opacity, yh[b, 1], lanes)
        sides = jnp.where(even, -half[2][0], half[2][1]) * lookup(opacity, jnp.where(even, zh[b, 0], zh[b, 1]), lanes)
        colour = [[None] * per for _ in range(3)]
        for x in span:
            for h in range(per):
                at = pl.ds(h * 8, 8)
                v = x * per + h
                g_x = 0.5 * (dens[b * depth + x + 2, at, :] - dens[b * depth + x, at, :])
                g_y = inner[b, 0, x, at, :]
                if h == 0:
                    g_y = jnp.where(line == 0, g_y - half_up[x:x + 1, :], g_y)
                if h == per - 1:
                    g_y = jnp.where(line == 7, g_y + half_down[x:x + 1, :], g_y)
                side = pltpu.roll(sides, lanes - 2 * v, 1) if v else sides
                g_z = inner[b, 1, x, at, :]
                g_z = jnp.where(on_side, g_z + side, g_z)
                facing = jnp.abs(g_x * LIGHT[0] + g_y * LIGHT[1] + g_z * LIGHT[2]) * lax.rsqrt(
                    1.0 + (g_x * g_x + g_y * g_y + g_z * g_z)
                )
                lit = 0.35 + 0.65 * facing
                for c in range(3):
                    term = wemit[b, c, x, at, :] * lit
                    colour[c][h] = term if colour[c][h] is None else colour[c][h] + term
        return [jnp.where(inside(b), jnp.concatenate(c, axis=0), 0.0) for c in colour]

    prepare(ix)

    def image_copy(buf, off, s_sem, r_sem):
        return pltpu.make_async_remote_copy(
            src_ref=buf.at[ix], dst_ref=buf.at[ix], send_sem=s_sem.at[off], recv_sem=r_sem.at[off],
            device_id={"gx": lax.rem(ix + off, n)}, device_id_type=MESH,
        )

    def for_images(act):
        for far in range(n - 1, 0, -1):
            @pl.when(ix + far < n)
            def _():
                act(far)

            @pl.when((ix - far >= 1) | ((ix == far) & (far < raw_from)))
            def _():
                act(n - far)

    @pl.when(ix < n - 2)
    def _():
        pl.semaphore_wait(far_ready, n - 2 - ix)
    for_images(lambda off: image_copy(alphas, off, a_send, a_recv).start())

    for a in range(3):
        @pl.when(has_lower[a])
        def _():
            halo_copy(a, 1).wait_recv()

        @pl.when(has_upper[a])
        def _():
            halo_copy(a, 0).wait_recv()
    opacity = table_ref[3:4, :]
    dens[ix * depth] = 2.0 * half[0][0] * lookup(opacity, xh[0], lanes)
    dens[ix * depth + depth + 1] = 2.0 * half[0][1] * lookup(opacity, xh[1], lanes)
    own = shade(ix, range(depth))
    for c in range(3):
        colours[ix, c] = own[c]
    for_images(lambda off: image_copy(colours, off, c_send, c_recv).start())
    loads[3].wait()

    @pl.when(ix == 0)
    def _():
        def step(b, carry):
            for which in range(2):
                pltpu.make_async_remote_copy(
                    src_ref=(vols, frames)[which].at[b], dst_ref=(vols, frames)[which].at[b],
                    send_sem=front_send.at[which], recv_sem=raw_recv.at[b, which],
                    device_id={"gx": 1}, device_id_type=MESH,
                ).wait_recv()
            prepare(b)
            for a, halo in ((1, yh), (2, zh)):
                for side, there in ((0, has_lower[a]), (1, has_upper[a])):
                    @pl.when(there)
                    def _():
                        pltpu.make_async_remote_copy(
                            src_ref=halo.at[b, side], dst_ref=halo.at[b, side],
                            send_sem=front_send.at[0], recv_sem=edge_recv.at[b, 2 * (a - 1) + side],
                            device_id={"gx": 1}, device_id_type=MESH,
                        ).wait_recv()

            @pl.when(b > raw_from)
            def _():
                rest = shade(b - 1, (depth - 1,))
                for c in range(3):
                    colours[b - 1, c] = colours[b - 1, c] + rest[c]
            got = shade(b, range(depth - 1))
            for c in range(3):
                colours[b, c] = got[c]
            return carry

        if raw_from > 1:
            pltpu.make_async_remote_copy(
                src_ref=vols.at[raw_from - 1, depth - 1], dst_ref=vols.at[raw_from - 1, depth - 1],
                send_sem=front_send.at[0], recv_sem=raw_recv.at[raw_from - 1, 0],
                device_id={"gx": 1}, device_id_type=MESH,
            ).wait_recv()
            dens[raw_from * depth] = lookup(opacity, vols[raw_from - 1, depth - 1], lanes)
        lax.fori_loop(raw_from, n, step, 0)
        if n > 1:
            dens[n * depth + 1] = jnp.zeros((rows, lanes), jnp.float32)
            rest = shade(n - 1, (depth - 1,))
            for c in range(3):
                colours[n - 1, c] = colours[n - 1, c] + rest[c]

    for off in range(1, n):
        @pl.when((ix > 0) | (n - off < raw_from))
        def _():
            image_copy(alphas, off, a_send, a_recv).wait_recv()

    clear = [1.0 - alphas[b] for b in range(n)]

    def cover(rank):
        seen = jnp.ones((rows, lanes), jnp.float32)
        for b in range(n):
            seen = seen * jnp.where(rank_ref[b] < rank, clear[b], 1.0)
        return seen

    own_cover = cover(rank_ref[ix])
    alpha = own_cover * alphas[ix]
    total = [own_cover * colours[ix, c] for c in range(3)]
    for off in range(1, n):
        b = lax.rem(ix + off, n)

        @pl.when((ix > 0) | (off < raw_from))
        def _():
            image_copy(colours, n - off, c_send, c_recv).wait_recv()
        seen = cover(rank_ref[b])
        alpha = alpha + seen * alphas[b]
        total = [total[c] + seen * colours[b, c] for c in range(3)]
    for c in range(3):
        out_ref[c] = total[c]
    out_ref[3] = alpha

    for a in range(3):
        @pl.when(has_lower[a])
        def _():
            halo_copy(a, 0).wait_send()

        @pl.when(has_upper[a])
        def _():
            halo_copy(a, 1).wait_send()
    for a in (1, 2):
        for side, there in ((0, has_lower[a]), (1, has_upper[a])):
            @pl.when(is_raw & there)
            def _():
                edge_to_front(a, side).wait_send()

    if raw_from > 1:
        @pl.when(ix == raw_from - 1)
        def _():
            last_to_front().wait_send()

    @pl.when(is_raw)
    def _():
        frame_to_front().wait_send()
        raw_to_front().wait_send()
    for_images(lambda off: image_copy(alphas, off, a_send, a_recv).wait_send())
    for_images(lambda off: image_copy(colours, off, c_send, c_recv).wait_send())


def on_device(sizes, volume, transfer_table, depth_rank, footprint):
    depth, rows, lanes = volume.shape
    n = sizes[0]
    vmem = pl.BlockSpec(memory_space=pltpu.VMEM)
    hbm = pl.BlockSpec(memory_space=pl.ANY)
    return pl.pallas_call(
        functools.partial(kernel, sizes),
        out_shape=pltpu.VMEM((4, rows, lanes), jnp.float32),
        in_specs=[hbm] * 4,
        out_specs=vmem,
        scratch_shapes=[
            pltpu.VMEM((n,) + volume.shape, jnp.int32),
            pltpu.VMEM(transfer_table.shape, jnp.float32),
            pltpu.SMEM(depth_rank.shape, jnp.int32),
            pltpu.SMEM(footprint.shape, jnp.int32),
            pltpu.SemaphoreType.DMA((4,)),
            pltpu.VMEM((n, 8, lanes), jnp.int32),
            pltpu.VMEM((2, depth, lanes), jnp.int32),
            pltpu.VMEM((2, 8, lanes), jnp.int32),
            pltpu.VMEM((2, rows, lanes), jnp.int32),
            pltpu.VMEM((n, 2, depth, lanes), jnp.int32),
            pltpu.VMEM((n, 2, 8, lanes), jnp.int32),
            pltpu.VMEM((n * depth + 2, rows, lanes), jnp.float32),
            pltpu.VMEM((n, 3, depth, rows, lanes), jnp.float32),
            pltpu.VMEM((n, 2, depth, rows, lanes), jnp.float32),
            pltpu.VMEM((n, rows, lanes), jnp.float32),
            pltpu.VMEM((n, 3, rows, lanes), jnp.float32),
            pltpu.SemaphoreType.REGULAR,
            pltpu.SemaphoreType.REGULAR,
            pltpu.SemaphoreType.DMA((3, 2)),
            pltpu.SemaphoreType.DMA((3, 2)),
            pltpu.SemaphoreType.DMA((6,)),
            pltpu.SemaphoreType.DMA((n, 2)),
            pltpu.SemaphoreType.DMA((n, 4)),
            pltpu.SemaphoreType.DMA((n,)),
            pltpu.SemaphoreType.DMA((n,)),
            pltpu.SemaphoreType.DMA((n,)),
            pltpu.SemaphoreType.DMA((n,)),
        ],
        compiler_params=pltpu.CompilerParams(collective_id=0, has_side_effects=True),
        name="raycast",
    )(volume, transfer_table, depth_rank, footprint)


def solution(mesh):
    placed = (P("gx", "gy", "gz"), P(), P(), P("gx", "gy", "gz", None))
    sizes = tuple(mesh.shape[a] for a in AXES)
    return jax.shard_map(
        functools.partial(on_device, sizes), mesh=mesh, in_specs=placed,
        out_specs=P(None, "gy", "gz"), check_vma=False,
    )
```

time: 12.6 us -> 11.6 us (0.921)
  Pallas kernels: 11.8 us -> 10.9 us
    pallas_call x1, Pallas kernels: 11.8 us -> 10.9 us  [on_device(): pl.pallas_call(functools.partial(kernel, sizes), out_shape=pltpu.VMEM((4,...]
where the time goes in v1:
time: 11.6 us; the launch traced here: 11.5 us
  Pallas kernels  10.9 us (94%)
  local copies, waits for them, and re-layouts  0.62 us (5%)
    pallas_call x1, Pallas kernels, on_device(): pl.pallas_call(functools.partial(kernel, sizes), out_shape=pltpu.VMEM((4,...  10.9 us
    unnamed x1, local copies, waits for them, and re-layouts  0.62 us

profile of v1, /device:TPU:0, one launch (start us, length us, event | category | flops | bytes accessed | tf_op | source)
XLA Modules:
  0.0 11.5 jit_solution(8479667829287470887)
XLA Ops:
  0.0 10.9 %raycast.1 = f32[4,16,128]{2,1,0:T(8,128)S(1)} custom-call(s32[8,16,128]{2,1,0:T(8,128)} %vol_hbm.1, f32[4,256]{1,0:T(4,128)} %table_hbm.1, s32[4]{0:T(128)} %rank_hbm.1, s32[1,1,1,4]{3,2,1,0:T(1,128)} %foot_hbm.1), custom_call_target="tpu_custom_call" | custom-call | tf_op jit(solution)/shard_map/raycast/pallas_call | solution.py:422
  10.9 0.6 %copy.6 = f32[4,16,128]{2,1,0:T(8,128)} copy(f32[4,16,128]{2,1,0:T(8,128)S(1)} %raycast.1) | data formatting | bytes 65536

commit v2 on v1

--- a/solution.py
+++ b/solution.py
@@ -10,7 +10,6 @@
 LIGHT = (1.0 / 3.0, 2.0 / 3.0, 2.0 / 3.0)
 AXES = ("gx", "gy", "gz")
 MESH = pl.DeviceIdType.MESH
-RAW = 1
 
 
 def lookup(table_row, index, lanes):
@@ -34,8 +33,19 @@
     extent = 4.0 / (depth * n)
     me = [lax.axis_index(a) for a in AXES]
     ix = me[0]
-    raw_from = max(1, n - RAW)
+
+    def first_raw(gy, gz):
+        even = 1 - lax.rem(gy + 2, 2)
+        return lax.max(1, n - even * (2 - lax.min(gy + gz, 1)))
+
+    raw_from = first_raw(me[1], me[2])
     is_raw = ix >= raw_from
+
+    def wants_edge(a, side):
+        step = 1 if side else -1
+        gy, gz = me[1] + (step if a == 1 else 0), me[2] + (step if a == 2 else 0)
+        return (has_upper if side else has_lower)[a] & (ix >= first_raw(gy, gz))
+
     has_lower = [me[a] > 0 for a in range(3)]
     has_upper = [me[a] < sizes[a] - 1 for a in range(3)]
 
@@ -106,11 +116,81 @@
     row_no = lax.broadcasted_iota(jnp.int32, (rows, lanes), 0)
     lane_no = lax.broadcasted_iota(jnp.int32, (rows, lanes), 1)
 
+    sources = (
+        (vols.at[ix, 0], vols.at[ix, depth - 1]),
+        (yedge.at[0], yedge.at[1]),
+        (zedge.at[0], zedge.at[1]),
+    )
+
+    def landing(a, side):
+        return xh.at[1 - side] if a == 0 else (None, yh, zh)[a].at[ix, 1 - side]
+
+    def halo_copy(a, side):
+        return pltpu.make_async_remote_copy(
+            src_ref=sources[a][side], dst_ref=landing(a, side),
+            send_sem=halo_send.at[a, side], recv_sem=halo_recv.at[a, 1 - side],
+            device_id={AXES[a]: me[a] + (1 if side else -1)}, device_id_type=MESH,
+        )
+
+    def edge_to_front(a, side):
+        return pltpu.make_async_remote_copy(
+            src_ref=sources[a][side], dst_ref=landing(a, side),
+            send_sem=front_send.at[2 * a + side], recv_sem=edge_recv.at[ix, 2 * (a - 1) + 1 - side],
+            device_id={"gx": 0, AXES[a]: me[a] + (1 if side else -1)}, device_id_type=MESH,
+        )
+
+    def raw_to_front():
+        return pltpu.make_async_remote_copy(
+            src_ref=vols.at[ix], dst_ref=vols.at[ix], send_sem=front_send.at[0], recv_sem=raw_recv.at[ix, 0],
+            device_id={"gx": 0}, device_id_type=MESH,
+        )
+
+    def last_to_front():
+        k = raw_from - 1
+        return pltpu.make_async_remote_copy(
+            src_ref=vols.at[k, depth - 1], dst_ref=vols.at[k, depth - 1],
+            send_sem=front_send.at[0], recv_sem=raw_recv.at[k, 0],
+            device_id={"gx": 0}, device_id_type=MESH,
+        )
+
+    def frame_to_front():
+        return pltpu.make_async_remote_copy(
+            src_ref=frames.at[ix], dst_ref=frames.at[ix], send_sem=front_send.at[1], recv_sem=raw_recv.at[ix, 1],
+            device_id={"gx": 0}, device_id_type=MESH,
+        )
+
     loads[0].wait()
+
+    @pl.when(has_lower[0])
+    def _():
+        halo_copy(0, 0).start()
+
+    def send_raw(when):
+        @pl.when(when & (ix > 0) & (ix == raw_from - 1) & (raw_from < n))
+        def _():
+            last_to_front().start()
+
+        @pl.when(when & is_raw)
+        def _():
+            raw_to_front().start()
+
+    at_first = me[1] + me[2] == 0
+    send_raw(at_first)
     vol3 = vols[ix]
     vol = vol3.reshape(depth * rows, lanes)
     yedge[0] = vol3[:, 0, :]
     yedge[1] = vol3[:, rows - 1, :]
+
+    def send_lower(a):
+        @pl.when(wants_edge(a, 0))
+        def _():
+            edge_to_front(a, 0).start()
+
+        @pl.when(has_lower[a])
+        def _():
+            halo_copy(a, 0).start()
+
+    send_lower(1)
     first = jnp.zeros((8, lanes), jnp.int32)
     last = jnp.zeros((8, lanes), jnp.int32)
     for v in range(depth * per):
@@ -121,67 +201,8 @@
         first = jnp.where(lane == to_first, pltpu.roll(piece, to_first, 1) if to_first else piece, first)
     zedge[0] = first
     zedge[1] = last
-    sources = (
-        (vols.at[ix, 0], vols.at[ix, depth - 1]),
-        (yedge.at[0], yedge.at[1]),
-        (zedge.at[0], zedge.at[1]),
-    )
-
-    def landing(a, side):
-        return xh.at[1 - side] if a == 0 else (None, yh, zh)[a].at[ix, 1 - side]
-
-    def halo_copy(a, side):
-        return pltpu.make_async_remote_copy(
-            src_ref=sources[a][side], dst_ref=landing(a, side),
-            send_sem=halo_send.at[a, side], recv_sem=halo_recv.at[a, 1 - side],
-            device_id={AXES[a]: me[a] + (1 if side else -1)}, device_id_type=MESH,
-        )
-
-    def edge_to_front(a, side):
-        return pltpu.make_async_remote_copy(
-            src_ref=sources[a][side], dst_ref=landing(a, side),
-            send_sem=front_send.at[2 * a + side], recv_sem=edge_recv.at[ix, 2 * (a - 1) + 1 - side],
-            device_id={"gx": 0, AXES[a]: me[a] + (1 if side else -1)}, device_id_type=MESH,
-        )
-
-    def raw_to_front():
-        return pltpu.make_async_remote_copy(
-            src_ref=vols.at[ix], dst_ref=vols.at[ix], send_sem=front_send.at[0], recv_sem=raw_recv.at[ix, 0],
-            device_id={"gx": 0}, device_id_type=MESH,
-        )
-
-    def last_to_front():
-        k = raw_from - 1
-        return pltpu.make_async_remote_copy(
-            src_ref=vols.at[k, depth - 1], dst_ref=vols.at[k, depth - 1],
-            send_sem=front_send.at[0], recv_sem=raw_recv.at[k, 0],
-            device_id={"gx": 0}, device_id_type=MESH,
-        )
-
-    def frame_to_front():
-        return pltpu.make_async_remote_copy(
-            src_ref=frames.at[ix], dst_ref=frames.at[ix], send_sem=front_send.at[1], recv_sem=raw_recv.at[ix, 1],
-            device_id={"gx": 0}, device_id_type=MESH,
-        )
-
-    for a in (2, 1):
-        @pl.when(is_raw & has_lower[a])
-        def _():
-            edge_to_front(a, 0).start()
-    for a in (0, 2, 1):
-        @pl.when(has_lower[a])
-        def _():
-            halo_copy(a, 0).start()
-
-    if raw_from > 1:
-        @pl.when(ix == raw_from - 1)
-        def _():
-            last_to_front().start()
-
-    @pl.when(is_raw)
-    def _():
-        raw_to_front().start()
-
+    send_lower(2)
+    send_raw(jnp.logical_not(at_first))
     loads[2].wait()
     frames[ix] = jnp.where(
         line == 0,
@@ -206,7 +227,7 @@
         def _():
             halo_copy(a, 1).start()
     for a in (2, 1):
-        @pl.when(is_raw & has_upper[a])
+        @pl.when(wants_edge(a, 1))
         def _():
             edge_to_front(a, 1).start()
 
@@ -314,7 +335,7 @@
     for_images(lambda off: image_copy(colours, off, c_send, c_recv).start())
     loads[3].wait()
 
-    @pl.when(ix == 0)
+    @pl.when((ix == 0) & (raw_from < n))
     def _():
         def step(b, carry):
             for which in range(2):
@@ -344,7 +365,8 @@
                 colours[b, c] = got[c]
             return carry
 
-        if raw_from > 1:
+        @pl.when(raw_from > 1)
+        def _():
             pltpu.make_async_remote_copy(
                 src_ref=vols.at[raw_from - 1, depth - 1], dst_ref=vols.at[raw_from - 1, depth - 1],
                 send_sem=front_send.at[0], recv_sem=raw_recv.at[raw_from - 1, 0],
@@ -352,11 +374,10 @@
             ).wait_recv()
             dens[raw_from * depth] = lookup(opacity, vols[raw_from - 1, depth - 1], lanes)
         lax.fori_loop(raw_from, n, step, 0)
-        if n > 1:
-            dens[n * depth + 1] = jnp.zeros((rows, lanes), jnp.float32)
-            rest = shade(n - 1, (depth - 1,))
-            for c in range(3):
-                colours[n - 1, c] = colours[n - 1, c] + rest[c]
+        dens[n * depth + 1] = jnp.zeros((rows, lanes), jnp.float32)
+        rest = shade(n - 1, (depth - 1,))
+        for c in range(3):
+            colours[n - 1, c] = colours[n - 1, c] + rest[c]
 
     for off in range(1, n):
         @pl.when((ix > 0) | (n - off < raw_from))
@@ -371,21 +392,20 @@
             seen = seen * jnp.where(rank_ref[b] < rank, clear[b], 1.0)
         return seen
 
-    own_cover = cover(rank_ref[ix])
-    alpha = own_cover * alphas[ix]
-    total = [own_cover * colours[ix, c] for c in range(3)]
+    order = [lax.rem(ix + off, n) for off in range(n)]
+    covers = [cover(rank_ref[b]) for b in order]
+    alpha = covers[0] * alphas[ix]
     for off in range(1, n):
-        b = lax.rem(ix + off, n)
-
+        alpha = alpha + covers[off] * alphas[order[off]]
+    out_ref[3] = alpha
+    total = [covers[0] * colours[ix, c] for c in range(3)]
+    for off in range(1, n):
         @pl.when((ix > 0) | (off < raw_from))
         def _():
             image_copy(colours, n - off, c_send, c_recv).wait_recv()
-        seen = cover(rank_ref[b])
-        alpha = alpha + seen * alphas[b]
-        total = [total[c] + seen * colours[b, c] for c in range(3)]
+        total = [total[c] + covers[off] * colours[order[off], c] for c in range(3)]
     for c in range(3):
         out_ref[c] = total[c]
-    out_ref[3] = alpha
 
     for a in range(3):
         @pl.when(has_lower[a])
@@ -396,15 +416,14 @@
         def _():
             halo_copy(a, 1).wait_send()
     for a in (1, 2):
-        for side, there in ((0, has_lower[a]), (1, has_upper[a])):
-            @pl.when(is_raw & there)
+        for side in range(2):
+            @pl.when(wants_edge(a, side))
             def _():
                 edge_to_front(a, side).wait_send()
 
-    if raw_from > 1:
-        @pl.when(ix == raw_from - 1)
-        def _():
-            last_to_front().wait_send()
+    @pl.when((ix > 0) & (ix == raw_from - 1) & (raw_from < n))
+    def _():
+        last_to_front().wait_send()
 
     @pl.when(is_raw)
     def _():

time: 11.6 us -> 10.9 us (0.940)
  the two profiles are of different devices: /device:TPU:0 before, /device:TPU:1 now
where the time goes in v2:
time: 10.9 us; the launch traced here: 10.7 us
  Pallas kernels  10.1 us (93%)
  local copies, waits for them, and re-layouts  0.62 us (6%)
    pallas_call x1, Pallas kernels, on_device(): pl.pallas_call(functools.partial(kernel, sizes), out_shape=pltpu.VMEM((4,...  10.1 us
    unnamed x1, local copies, waits for them, and re-layouts  0.62 us

profile of v2, /device:TPU:1, one launch (start us, length us, event | category | flops | bytes accessed | tf_op | source)
XLA Modules:
  0.0 10.7 jit_solution(9364353854204704971)
XLA Ops:
  0.0 10.1 %raycast.1 = f32[4,16,128]{2,1,0:T(8,128)S(1)} custom-call(s32[8,16,128]{2,1,0:T(8,128)} %vol_hbm.1, f32[4,256]{1,0:T(4,128)} %table_hbm.1, s32[4]{0:T(128)} %rank_hbm.1, s32[1,1,1,4]{3,2,1,0:T(1,128)} %foot_hbm.1), custom_call_target="tpu_custom_call" | custom-call | tf_op jit(solution)/shard_map/raycast/pallas_call | solution.py:441
  10.1 0.6 %copy.6 = f32[4,16,128]{2,1,0:T(8,128)} copy(f32[4,16,128]{2,1,0:T(8,128)S(1)} %raycast.1) | data formatting | bytes 65536

commit v3 on v2

--- a/solution.py
+++ b/solution.py
@@ -12,19 +12,20 @@
 MESH = pl.DeviceIdType.MESH
 
 
-def lookup(table_row, index, lanes):
-    entries = table_row.shape[1]
+def lookup(table, index, lanes):
+    count, entries = table.shape
     low = index & (lanes - 1)
-    found = None
+    found = [None] * count
     for part in range(entries // lanes):
-        piece = jnp.broadcast_to(table_row[:, part * lanes:(part + 1) * lanes], index.shape)
-        got = jnp.take_along_axis(piece, low, axis=1, mode="promise_in_bounds")
-        found = got if found is None else jnp.where(index >= part * lanes, got, found)
+        for t in range(count):
+            piece = jnp.broadcast_to(table[t:t + 1, part * lanes:(part + 1) * lanes], index.shape)
+            got = jnp.take_along_axis(piece, low, axis=1, mode="promise_in_bounds")
+            found[t] = got if part == 0 else jnp.where(index >= part * lanes, got, found[t])
     return found
 
 
 def kernel(sizes, vol_hbm, table_hbm, rank_hbm, foot_hbm, out_ref,
-           vols, table_ref, rank_ref, foot_ref, load_sem, frames, yedge, zedge, xh, yh, zh,
+           vols, table_ref, rank_ref, foot_ref, load_sem, frames, zedge, xh, yh, zh,
            dens, wemit, inner, alphas, colours,
            ready, far_ready, halo_send, halo_recv, front_send, raw_recv, edge_recv, a_send, a_recv, c_send, c_recv):
     n, ny, nz = sizes
@@ -36,7 +37,7 @@
 
     def first_raw(gy, gz):
         even = 1 - lax.rem(gy + 2, 2)
-        return lax.max(1, n - even * (2 - lax.min(gy + gz, 1)))
+        return lax.max(1, n - even * (3 - 2 * lax.min(gy + gz, 1)))
 
     raw_from = first_raw(me[1], me[2])
     is_raw = ix >= raw_from
@@ -51,22 +52,6 @@
 
     def signal(sem, **where):
         pl.semaphore_signal(sem, inc=1, device_id=where, device_id_type=MESH)
-
-    barrier = pltpu.get_barrier_semaphore()
-    for off in range(n - 1, 0, -1):
-        @pl.when(ix + off < n)
-        def _():
-            signal(barrier, gx=ix + off)
-    for a in (1, 2):
-        if sizes[a] > 1:
-            @pl.when(has_upper[a])
-            def _():
-                signal(barrier, **{AXES[a]: me[a] + 1})
-
-            @pl.when((ix == 0) & has_upper[a])
-            def _():
-                for k in range(n - 1, 0, -1):
-                    signal(barrier, **{"gx": k, AXES[a]: me[a] + 1})
 
     loads = [
         pltpu.make_async_copy(src, dst, load_sem.at[i])
@@ -77,6 +62,22 @@
     for load in loads:
         load.start()
 
+    barrier = pltpu.get_barrier_semaphore()
+    for off in range(n - 1, 0, -1):
+        @pl.when(ix + off < n)
+        def _():
+            signal(barrier, gx=ix + off)
+    for a in (1, 2):
+        if sizes[a] > 1:
+            @pl.when(has_upper[a])
+            def _():
+                signal(barrier, **{AXES[a]: me[a] + 1})
+
+            @pl.when((ix == 0) & has_upper[a])
+            def _():
+                for k in range(n - 1, 0, -1):
+                    signal(barrier, **{"gx": k, AXES[a]: me[a] + 1})
+
     greeted = ix
     for a in (1, 2):
         greeted = greeted + lax.min(me[a], 1) * (1 + lax.min(ix, 1))
@@ -89,7 +90,7 @@
         if sizes[a] > 1:
             @pl.when(has_lower[a])
             def _():
-                signal(ready, **{AXES[a]: me[a] - 1})
+                signal(ready.at[a], **{AXES[a]: me[a] - 1})
     for off in range(2, n):
         @pl.when(ix - off >= 0)
         def _():
@@ -118,7 +119,7 @@
 
     sources = (
         (vols.at[ix, 0], vols.at[ix, depth - 1]),
-        (yedge.at[0], yedge.at[1]),
+        (vols.at[ix, :, 0], vols.at[ix, :, rows - 1]),
         (zedge.at[0], zedge.at[1]),
     )
 
@@ -178,8 +179,6 @@
     send_raw(at_first)
     vol3 = vols[ix]
     vol = vol3.reshape(depth * rows, lanes)
-    yedge[0] = vol3[:, 0, :]
-    yedge[1] = vol3[:, rows - 1, :]
 
     def send_lower(a):
         @pl.when(wants_edge(a, 0))
@@ -214,17 +213,10 @@
     def _():
         frame_to_front().start()
 
-    above = 0
-    for a in range(3):
-        above = above + lax.min(sizes[a] - 1 - me[a], 1)
-
-    @pl.when(above > 0)
-    def _():
-        pl.semaphore_wait(ready, above)
-
-    for a in (0, 2, 1):
+    for a in (0, 1, 2):
         @pl.when(has_upper[a])
         def _():
+            pl.semaphore_wait(ready.at[a], 1)
             halo_copy(a, 1).start()
     for a in (2, 1):
         @pl.when(wants_edge(a, 1))
@@ -238,20 +230,18 @@
         return (frame[0:1] > 0) & (row_no >= frame[1:2]) & (row_no < frame[2:3])
 
     def prepare(b):
-        ints = vols[b].reshape(depth * rows, lanes)
-        d3 = lookup(table_ref[3:4, :], ints, lanes).reshape(depth, rows, lanes)
-        dens[pl.ds(b * depth + 1, depth)] = d3
         transmit = jnp.ones((rows, lanes), jnp.float32)
-        weights = []
+        d3 = []
         for x in range(depth):
+            found = lookup(table_ref, vols[b, x], lanes)
+            d3.append(found[3])
+            dens[b * depth + x + 1] = d3[x]
             sample = 1.0 - jnp.exp(-extent * d3[x])
-            weights.append(transmit * sample)
+            weight = transmit * sample
             transmit = transmit * (1.0 - sample)
+            for c in range(3):
+                wemit[b, c, x] = weight * found[c]
         alphas[b] = jnp.where(inside(b), 1.0 - transmit, 0.0)
-        for c in range(3):
-            emit = lookup(table_ref[c:c + 1, :], ints, lanes).reshape(depth, rows, lanes)
-            for x in range(depth):
-                wemit[b, c, x] = weights[x] * emit[x]
         for x in range(depth):
             d = d3[x]
             up = jnp.where(row_no == 0, 0.0, pltpu.roll(d, 1, 0))
@@ -269,9 +259,9 @@
 
     def shade(b, span):
         opacity = table_ref[3:4, :]
-        half_up = half[1][0] * lookup(opacity, yh[b, 0], lanes)
-        half_down = half[1][1] * lookup(opacity, yh[b, 1], lanes)
-        sides = jnp.where(even, -half[2][0], half[2][1]) * lookup(opacity, jnp.where(even, zh[b, 0], zh[b, 1]), lanes)
+        half_up = half[1][0] * lookup(opacity, yh[b, 0], lanes)[0]
+        half_down = half[1][1] * lookup(opacity, yh[b, 1], lanes)[0]
+        sides = jnp.where(even, -half[2][0], half[2][1]) * lookup(opacity, jnp.where(even, zh[b, 0], zh[b, 1]), lanes)[0]
         colour = [[None] * per for _ in range(3)]
         for x in span:
             for h in range(per):
@@ -327,8 +317,8 @@
         def _():
             halo_copy(a, 0).wait_recv()
     opacity = table_ref[3:4, :]
-    dens[ix * depth] = 2.0 * half[0][0] * lookup(opacity, xh[0], lanes)
-    dens[ix * depth + depth + 1] = 2.0 * half[0][1] * lookup(opacity, xh[1], lanes)
+    dens[ix * depth] = 2.0 * half[0][0] * lookup(opacity, xh[0], lanes)[0]
+    dens[ix * depth + depth + 1] = 2.0 * half[0][1] * lookup(opacity, xh[1], lanes)[0]
     own = shade(ix, range(depth))
     for c in range(3):
         colours[ix, c] = own[c]
@@ -355,15 +345,22 @@
                             device_id={"gx": 1}, device_id_type=MESH,
                         ).wait_recv()
 
-            @pl.when(b > raw_from)
-            def _():
-                rest = shade(b - 1, (depth - 1,))
+            def cast(span, follows):
+                got = shade(b, span)
+                rest = shade(b - 1, (depth - 1,)) if follows else None
                 for c in range(3):
-                    colours[b - 1, c] = colours[b - 1, c] + rest[c]
-            got = shade(b, range(depth - 1))
-            for c in range(3):
-                colours[b, c] = got[c]
+                    colours[b, c] = got[c]
+                    if follows:
+                        colours[b - 1, c] = colours[b - 1, c] + rest[c]
+
+            for is_last, span in ((False, range(depth - 1)), (True, range(depth))):
+                for follows in (False, True):
+                    @pl.when(((b == n - 1) == is_last) & ((b > raw_from) == follows))
+                    def _():
+                        cast(span, follows)
             return carry
+
+        dens[n * depth + 1] = jnp.zeros((rows, lanes), jnp.float32)
 
         @pl.when(raw_from > 1)
         def _():
@@ -372,12 +369,8 @@
                 send_sem=front_send.at[0], recv_sem=raw_recv.at[raw_from - 1, 0],
                 device_id={"gx": 1}, device_id_type=MESH,
             ).wait_recv()
-            dens[raw_from * depth] = lookup(opacity, vols[raw_from - 1, depth - 1], lanes)
+            dens[raw_from * depth] = lookup(opacity, vols[raw_from - 1, depth - 1], lanes)[0]
         lax.fori_loop(raw_from, n, step, 0)
-        dens[n * depth + 1] = jnp.zeros((rows, lanes), jnp.float32)
-        rest = shade(n - 1, (depth - 1,))
-        for c in range(3):
-            colours[n - 1, c] = colours[n - 1, c] + rest[c]
 
     for off in range(1, n):
         @pl.when((ix > 0) | (n - off < raw_from))
@@ -398,6 +391,31 @@
     for off in range(1, n):
         alpha = alpha + covers[off] * alphas[order[off]]
     out_ref[3] = alpha
+    for a in range(3):
+        @pl.when(has_lower[a])
+        def _():
+            halo_copy(a, 0).wait_send()
+
+        @pl.when(has_upper[a])
+        def _():
+            halo_copy(a, 1).wait_send()
+    for a in (1, 2):
+        for side in range(2):
+            @pl.when(wants_edge(a, side))
+            def _():
+                edge_to_front(a, side).wait_send()
+
+    @pl.when((ix > 0) & (ix == raw_from - 1) & (raw_from < n))
+    def _():
+        last_to_front().wait_send()
+
+    @pl.when(is_raw)
+    def _():
+        frame_to_front().wait_send()
+        raw_to_front().wait_send()
+    for_images(lambda off: image_copy(alphas, off, a_send, a_recv).wait_send())
+    for_images(lambda off: image_copy(colours, off, c_send, c_recv).wait_send())
+
     total = [covers[0] * colours[ix, c] for c in range(3)]
     for off in range(1, n):
         @pl.when((ix > 0) | (off < raw_from))
@@ -406,31 +424,6 @@
         total = [total[c] + covers[off] * colours[order[off], c] for c in range(3)]
     for c in range(3):
         out_ref[c] = total[c]
-
-    for a in range(3):
-        @pl.when(has_lower[a])
-        def _():
-            halo_copy(a, 0).wait_send()
-
-        @pl.when(has_upper[a])
-        def _():
-            halo_copy(a, 1).wait_send()
-    for a in (1, 2):
-        for side in range(2):
-            @pl.when(wants_edge(a, side))
-            def _():
-                edge_to_front(a, side).wait_send()
-
-    @pl.when((ix > 0) & (ix == raw_from - 1) & (raw_from < n))
-    def _():
-        last_to_front().wait_send()
-
-    @pl.when(is_raw)
-    def _():
-        frame_to_front().wait_send()
-        raw_to_front().wait_send()
-    for_images(lambda off: image_copy(alphas, off, a_send, a_recv).wait_send())
-    for_images(lambda off: image_copy(colours, off, c_send, c_recv).wait_send())
 
 
 def on_device(sizes, volume, transfer_table, depth_rank, footprint):
@@ -450,7 +443,6 @@
             pltpu.SMEM(footprint.shape, jnp.int32),
             pltpu.SemaphoreType.DMA((4,)),
             pltpu.VMEM((n, 8, lanes), jnp.int32),
-            pltpu.VMEM((2, depth, lanes), jnp.int32),
             pltpu.VMEM((2, 8, lanes), jnp.int32),
             pltpu.VMEM((2, rows, lanes), jnp.int32),
             pltpu.VMEM((n, 2, depth, lanes), jnp.int32),
@@ -460,7 +452,7 @@
             pltpu.VMEM((n, 2, depth, rows, lanes), jnp.float32),
             pltpu.VMEM((n, rows, lanes), jnp.float32),
             pltpu.VMEM((n, 3, rows, lanes), jnp.float32),
-            pltpu.SemaphoreType.REGULAR,
+            pltpu.SemaphoreType.REGULAR((3,)),
             pltpu.SemaphoreType.REGULAR,
             pltpu.SemaphoreType.DMA((3, 2)),
             pltpu.SemaphoreType.DMA((3, 2)),

time: 10.9 us -> 10.8 us (level)
  no operation moved by 1% of the time
where the time goes in v3:
time: 10.8 us; the launch traced here: 10.7 us
  Pallas kernels  10.1 us (94%)
  local copies, waits for them, and re-layouts  0.62 us (6%)
    pallas_call x1, Pallas kernels, on_device(): pl.pallas_call(functools.partial(kernel, sizes), out_shape=pltpu.VMEM((4,...  10.1 us
    unnamed x1, local copies, waits for them, and re-layouts  0.62 us

profile of v3, /device:TPU:1, one launch (start us, length us, event | category | flops | bytes accessed | tf_op | source)
XLA Modules:
  0.0 10.7 jit_solution(3301566967436163806)
XLA Ops:
  0.0 10.1 %raycast.1 = f32[4,16,128]{2,1,0:T(8,128)S(1)} custom-call(s32[8,16,128]{2,1,0:T(8,128)} %vol_hbm.1, f32[4,256]{1,0:T(4,128)} %table_hbm.1, s32[4]{0:T(128)} %rank_hbm.1, s32[1,1,1,4]{3,2,1,0:T(1,128)} %foot_hbm.1), custom_call_target="tpu_custom_call" | custom-call | tf_op jit(solution)/shard_map/raycast/pallas_call | solution.py:434
  10.1 0.6 %copy.6 = f32[4,16,128]{2,1,0:T(8,128)} copy(f32[4,16,128]{2,1,0:T(8,128)S(1)} %raycast.1) | data formatting | bytes 65536

commit v4 on v3

--- a/solution.py
+++ b/solution.py
@@ -53,13 +53,17 @@
     def signal(sem, **where):
         pl.semaphore_signal(sem, inc=1, device_id=where, device_id_type=MESH)
 
+    cut = max(1, depth // 2)
+    head, rest = pl.ds(0, cut), pl.ds(cut, depth - cut)
     loads = [
         pltpu.make_async_copy(src, dst, load_sem.at[i])
         for i, (src, dst) in enumerate((
-            (vol_hbm, vols.at[ix]), (table_hbm, table_ref), (foot_hbm, foot_ref), (rank_hbm, rank_ref)
+            (vol_hbm.at[head], vols.at[ix, head]), (table_hbm, table_ref), (foot_hbm, foot_ref), (rank_hbm, rank_ref),
+            (vol_hbm.at[rest], vols.at[ix, rest]),
         ))
     ]
-    for load in loads:
+    loads = loads if depth > cut else loads[:4]
+    for load in (loads[0], *loads[4:], *loads[1:4]):
         load.start()
 
     barrier = pltpu.get_barrier_semaphore()
@@ -165,6 +169,9 @@
     @pl.when(has_lower[0])
     def _():
         halo_copy(0, 0).start()
+
+    for load in loads[4:]:
+        load.wait()
 
     def send_raw(when):
         @pl.when(when & (ix > 0) & (ix == raw_from - 1) & (raw_from < n))
@@ -257,11 +264,15 @@
     even = (lane & 1) == 0
     on_side = (lane == 0) | (lane == lanes - 1)
 
-    def shade(b, span):
+    def sides_of(b):
+        ints = jnp.where(even, zh[b, 0], zh[b, 1])
+        return jnp.where(even, -half[2][0], half[2][1]) * lookup(table_ref[3:4, :], ints, lanes)[0]
+
+    def shade(b, span, sides=None):
+        sides = sides_of(b) if sides is None else sides
         opacity = table_ref[3:4, :]
         half_up = half[1][0] * lookup(opacity, yh[b, 0], lanes)[0]
         half_down = half[1][1] * lookup(opacity, yh[b, 1], lanes)[0]
-        sides = jnp.where(even, -half[2][0], half[2][1]) * lookup(opacity, jnp.where(even, zh[b, 0], zh[b, 1]), lanes)[0]
         colour = [[None] * per for _ in range(3)]
         for x in span:
             for h in range(per):
@@ -308,7 +319,7 @@
         pl.semaphore_wait(far_ready, n - 2 - ix)
     for_images(lambda off: image_copy(alphas, off, a_send, a_recv).start())
 
-    for a in range(3):
+    def await_halo(a):
         @pl.when(has_lower[a])
         def _():
             halo_copy(a, 1).wait_recv()
@@ -316,10 +327,15 @@
         @pl.when(has_upper[a])
         def _():
             halo_copy(a, 0).wait_recv()
+
+    await_halo(0)
     opacity = table_ref[3:4, :]
     dens[ix * depth] = 2.0 * half[0][0] * lookup(opacity, xh[0], lanes)[0]
     dens[ix * depth + depth + 1] = 2.0 * half[0][1] * lookup(opacity, xh[1], lanes)[0]
-    own = shade(ix, range(depth))
+    await_halo(2)
+    own_sides = sides_of(ix)
+    await_halo(1)
+    own = shade(ix, range(depth), own_sides)
     for c in range(3):
         colours[ix, c] = own[c]
     for_images(lambda off: image_copy(colours, off, c_send, c_recv).start())
@@ -441,7 +457,7 @@
             pltpu.VMEM(transfer_table.shape, jnp.float32),
             pltpu.SMEM(depth_rank.shape, jnp.int32),
             pltpu.SMEM(footprint.shape, jnp.int32),
-            pltpu.SemaphoreType.DMA((4,)),
+            pltpu.SemaphoreType.DMA((5,)),
             pltpu.VMEM((n, 8, lanes), jnp.int32),
             pltpu.VMEM((2, 8, lanes), jnp.int32),
             pltpu.VMEM((2, rows, lanes), jnp.int32),

time: 10.8 us -> 10.7 us (level)
  Pallas kernels: 10.1 us -> 9.93 us
    pallas_call x1, Pallas kernels: 10.1 us -> 9.93 us  [on_device(): pl.pallas_call(functools.partial(kernel, sizes), out_shape=pltpu.VMEM((4,...]
where the time goes in v4:
time: 10.7 us; the launch traced here: 10.6 us
  Pallas kernels  9.93 us (93%)
  local copies, waits for them, and re-layouts  0.62 us (6%)
    pallas_call x1, Pallas kernels, on_device(): pl.pallas_call(functools.partial(kernel, sizes), out_shape=pltpu.VMEM((4,...  9.93 us
    unnamed x1, local copies, waits for them, and re-layouts  0.62 us

profile of v4, /device:TPU:1, one launch (start us, length us, event | category | flops | bytes accessed | tf_op | source)
XLA Modules:
  0.0 10.6 jit_solution(4979678142325926913)
XLA Ops:
  0.0 9.9 %raycast.1 = f32[4,16,128]{2,1,0:T(8,128)S(1)} custom-call(s32[8,16,128]{2,1,0:T(8,128)} %vol_hbm.1, f32[4,256]{1,0:T(4,128)} %table_hbm.1, s32[4]{0:T(128)} %rank_hbm.1, s32[1,1,1,4]{3,2,1,0:T(1,128)} %foot_hbm.1), custom_call_target="tpu_custom_call" | custom-call | tf_op jit(solution)/shard_map/raycast/pallas_call | solution.py:450
  9.9 0.6 %copy.6 = f32[4,16,128]{2,1,0:T(8,128)} copy(f32[4,16,128]{2,1,0:T(8,128)S(1)} %raycast.1) | data formatting | bytes 65536
